TPU v7x, 128 devices: a whole 4x4x4 slice. The times are simulated.
128 devices in a mesh: gx: 4 (over y_hi, core), gy: 4 (over z), gz: 8 (over y_lo, x).
Axes of the slice: x: 4, y: 4 (y_hi: 2, y_lo: 2; y = y_hi * 2 + y_lo), z: 4, core: 2. Of those that a mesh axis runs over, the one named last changes fastest.
Arguments:
- inputs: bfloat16 [131072, 2048], P(('gx', 'gy', 'gz')), may hold values from -24 to 24
- cotangent: bfloat16 [131072, 4096], P(('gx', 'gy', 'gz')), may hold values from -0.016479492 to 0.016479492
- master: float32 [2048, 4096], P(('gx', 'gy', 'gz')), may hold values from -3 to 3
- accum: float32 [2048, 4096], P(('gx', 'gy', 'gz')), may hold values from 0.05 to 1
Outputs:
- new_master: float32 [2048, 4096], P(('gx', 'gy', 'gz'))
- new_accum: float32 [2048, 4096], P(('gx', 'gy', 'gz'))
All inputs are finite; a program needn't handle non-finite values.
Results may differ from a plain program's by a relative error of at most 0.0003.
Values sent between devices are 32-bit elements; how exact they have to be, the bound alone decides.
A program may use at most 128 MiB of HBM per device.

v0:
```python
import functools

import jax
import jax.numpy as jnp
from jax import lax
from jax.sharding import Mesh
from jax.sharding import PartitionSpec as P

D = 4096
ROWS = 2048
GZ = ("gz_0", "gz_1")
GX_GY = ("gx_0", "gx_1", "gy")
GX_GY_GZ = ("gx_0", "gx_1", "gy", "gz_0", "gz_1")


def cut_along(array, dim, peers):
    before, after = (array.shape[:dim], array.shape[dim + 1 :])
    return jnp.moveaxis(array.reshape(*before, peers, -1, *after), dim, 0)


def summed_on_arrival(array, axis, dim):
    parts = cut_along(array, dim, lax.axis_size(axis))
    arrived = lax.all_to_all(parts, axis, split_axis=0, concat_axis=0, tiled=True)
    return arrived.sum(axis=0)


def one_axis_at_a_time(array, axes):
    return functools.reduce(lax.psum, axes, array)


def shards(inputs, cotangent, master, accum):
    partial_value = lax.psum_scatter(
        lax.dot_general(
            inputs, cotangent, (((0,), (0,)), ((), ())), preferred_element_type=jnp.float32
        ),
        GX_GY,
        scatter_dimension=0,
        tiled=True,
    )
    gradient = summed_on_arrival(partial_value, GZ, 0)
    squares = one_axis_at_a_time(jnp.sum(gradient * gradient), GX_GY_GZ)
    limit = 0.5 * jnp.sqrt(jnp.float32(ROWS * D))
    factor = limit / jnp.maximum(jnp.sqrt(squares), limit)
    scaled = factor * gradient
    new_accum = accum + scaled * scaled
    new_master = master - 0.5 * scaled / jnp.sqrt(new_accum)
    return (new_master, new_accum)


def solution(mesh):
    finer = Mesh(
        mesh.devices.reshape(2, 2, mesh.shape["gy"], 2, 4), ("gx_0", "gx_1", "gy", "gz_0", "gz_1")
    )
    placed = (P(GX_GY_GZ, None), P(GX_GY_GZ, None), P(GX_GY_GZ, None), P(GX_GY_GZ, None))
    return jax.shard_map(
        shards,
        mesh=finer,
        in_specs=placed,
        out_specs=(P(GX_GY_GZ, None), P(GX_GY_GZ, None)),
        check_vma=False,
    )
```

profile of v0, /device:TPU:0, one launch (start us, length us, event | category | flops | bytes accessed | tf_op | source)
XLA Modules:
  0.0 357.7 jit_solution(2068077032767912066)
XLA Ops:
  7.2 0.0 reduce-scatter.2.cloned.1.call-start
  7.2 25.3 %fusion = f32[2048,4096]{1,0:T(8,128)} fusion(bf16[1024,2048]{1,0:T(8,128)(2,1)} %param.4, bf16[1024,4096]{1,0:T(8,128)(2,1)} %param.5), kind=kOutput, calls=%fused_computation.3 | convolution fusion | flops 17179869184 | bytes 46137344 | tf_op jit(solution)/shard_map/dot_general | solution.py:33
  32.5 0.0 copy-start
  32.5 0.0 copy-start.1
  32.5 0.0 reduce-scatter.2.cloned.1.call-update
  32.6 251.0 %reduce-scatter.2.cloned.1.call-done = f32[128,4096]{1,0:T(8,128)} async-done(((f32[2048,4096]{1,0:T(8,128)}), f32[128,4096]{1,0:T(8,128)}) %reduce-scatter.2.cloned.1.call-update) | async-done | bytes 2097168 | tf_op jit(solution)/shard_map/reduce_scatter | solution.py:32
  283.6 28.9 %all_to_all.5 = f32[8,16,4096]{2,1,0:T(8,128)S(1)} all-to-all(f32[8,16,4096]{2,1,0:T(8,128)} %bitcast.3), channel_id=1, replica_groups=mesh['gx_0'=2,'gx_1'=2,'gy'=4,'gz_0'=2,'gz_1'=4] {'gz_0','gz_1'}, dimensions={0} | all-to-all | bytes 4194304 | tf_op jit(solution)/shard_map/all_to_all | solution.py:23
  312.6 0.1 reduce_sum.18
  312.7 0.7 multiply_reduce_fusion
  313.3 7.0 %psum.35 = f32[]{:T(128)} all-reduce(f32[]{:T(128)} %multiply_reduce_fusion), channel_id=1, replica_groups=mesh['gx_0'=2,'gx_1'=2,'gy'=4,'gz_0'=2,'gz_1'=4] {'gx_0'}, use_global_device_ids=true, to_apply=%region_3.0 | all-reduce | flops 1 | bytes 8 | tf_op jit(solution)/shard_map/psum | solution.py:28
  320.4 3.1 psum.36
  323.5 10.8 %psum.37 = f32[]{:T(128)} all-reduce(f32[]{:T(128)} %psum.36), channel_id=1, replica_groups=mesh['gx_0'=2,'gx_1'=2,'gy'=4,'gz_0'=2,'gz_1'=4] {'gy'}, use_global_device_ids=true, to_apply=%region_5.0 | all-reduce | flops 1 | bytes 8 | tf_op jit(solution)/shard_map/psum | solution.py:28
  334.3 5.5 %psum.38 = f32[]{:T(128)} all-reduce(f32[]{:T(128)} %psum.37), channel_id=1, replica_groups=mesh['gx_0'=2,'gx_1'=2,'gy'=4,'gz_0'=2,'gz_1'=4] {'gz_0'}, use_global_device_ids=true, to_apply=%region_6.0 | all-reduce | flops 1 | bytes 8 | tf_op jit(solution)/shard_map/psum | solution.py:28
  339.8 9.4 %psum.39 = f32[]{:T(128)} all-reduce(f32[]{:T(128)} %psum.38), channel_id=1, replica_groups=mesh['gx_0'=2,'gx_1'=2,'gy'=4,'gz_0'=2,'gz_1'=4] {'gz_1'}, use_global_device_ids=true, to_apply=%region_7.0 | all-reduce | flops 1 | bytes 8 | tf_op jit(solution)/shard_map/psum | solution.py:28
  350.0 0.0 copy-done
  350.0 0.0 copy-done.1
  350.0 0.8 multiply_subtract_fusion
Async XLA Ops:
  7.2 276.5 %reduce-scatter.2.cloned.1.call-start = ((), (), s32[]{:S(2)}) async-start(), calls=%async_computation.2 | async-start | bytes 35651584 | tf_op jit(solution)/shard_map/reduce_scatter | solution.py:32
  32.5 317.5 %copy-start = (f32[16,4096]{1,0:T(8,128)S(1)}, f32[16,4096]{1,0:T(8,128)}, u32[]{:S(2)}) copy-start(f32[16,4096]{1,0:T(8,128)} %param.6) | copy-start | bytes 786436
  32.5 317.5 %copy-start.1 = (f32[16,4096]{1,0:T(8,128)S(1)}, f32[16,4096]{1,0:T(8,128)}, u32[]{:S(2)}) copy-start(f32[16,4096]{1,0:T(8,128)} %param.7) | copy-start | bytes 786436
Sparse Core Ops, SparseCore 0:
  32.7 250.8 reduce-scatter.1
where the time goes:
time: 358 us
  waiting for transfers between devices  251 us (70%)
  blocking collectives  64.8 us (18%)
  matrix products  25.3 us (7%)
  between operations  14.8 us (4%)
    reduce_scatter x1, waiting for transfers between devices, shards(): lax.psum_scatter(lax.dot_general(inputs, cotangent, (((0,), (0,)), ((), (...  251 us
    psum x5, blocking collectives, one_axis_at_a_time(): return functools.reduce(lax.psum, axes, array)  35.9 us
    all_to_all x1, blocking collectives, summed_on_arrival(): lax.all_to_all(parts, axis, split_axis=0, concat_axis=0, tiled=True)  28.9 us
    dot_general x1, matrix products, shards(): lax.dot_general(inputs, cotangent, (((0,), (0,)), ((), ())), preferred_el...  25.3 us
  transfers between devices with their start and end apart: 1, of which 1 were waited for; matrix products, arithmetic and copies ran while one was open for 0% of the time, Pallas kernels for 0%

commit v1 on v0

v1 whole, which is shorter than its diff:
```python
import jax
import jax.numpy as jnp
from jax import lax
from jax.experimental import pallas as pl
from jax.experimental.pallas import tpu as pltpu
from jax.sharding import PartitionSpec as P

MESH = pl.DeviceIdType.MESH

D = 4096
ROWS = 2048
TOKENS = 1024
W = 128
PORTIONS = 3
WIDE = PORTIONS * W
CHUNKS = 11
LAST = CHUNKS - 1
UNITS = 33
TILE = 256
ORDERS = (("x", "y", "z"), ("y", "z", "x"), ("z", "x", "y"))
COUNTS = (CHUNKS - 1, CHUNKS, CHUNKS)
LAGS = 6


def unit_of(p, k):
    over = k // LAST
    return 3 * k + 2 * over if p == 0 else 3 * k + p - over


def column_of(k):
    return pl.multiple_of((3 * k - k // LAST) * W, W)


def kernel(
    x_hbm, c_hbm, master_hbm, accum_hbm,
    new_master, new_accum,
    xv, xt, cv, stage, other, part, fwd1, got1, fwd2, got2, got3,
    grad, master, accum, squares, norm_out, norm_in,
    x_sem, c_sem, state_sem, stage_sem, other_sem, send_sem,
    fwd1_sem, got1_sem, fwd2_sem, got2_sem, got3_sem, norm_send, norm_recv,
):
    gx, gy, gz = lax.axis_index("gx"), lax.axis_index("gy"), lax.axis_index("gz")
    core = gx % 2
    me = {"x": gz % 4, "y": 2 * (gx // 2) + gz // 4, "z": gy}

    def device(axis=None, step=0, on=None):
        at = dict(me)
        if axis is not None:
            at[axis] = (at[axis] + step) % 4
        on = core if on is None else on
        return (2 * (at["y"] // 2) + on, at["z"], 4 * (at["y"] % 2) + at["x"])

    partner = device(on=1 - core)

    x_loads = []
    for j in range(4):
        whose = 1 - core if j < 2 else core
        at = pl.multiple_of((j % 2) * 1024 + whose * 512, 512)
        x_loads.append(
            pltpu.make_async_copy(x_hbm.at[:, pl.ds(at, 512)], xv.at[j], x_sem.at[j])
        )
    c_first = pltpu.make_async_copy(
        c_hbm.at[:, pl.ds(0, WIDE)], cv.at[:, pl.ds(0, WIDE)], c_sem.at[0]
    )
    c_rest = pltpu.make_async_copy(
        c_hbm.at[:, pl.ds(WIDE, D - WIDE)], cv.at[:, pl.ds(WIDE, D - WIDE)], c_sem.at[1]
    )
    state_loads = [
        pltpu.make_async_copy(master_hbm, master, state_sem.at[0]),
        pltpu.make_async_copy(accum_hbm, accum, state_sem.at[1]),
    ]
    x_loads[0].start()
    c_first.start()
    x_loads[1].start()
    x_loads[2].start()
    x_loads[3].start()

    barrier = pltpu.get_barrier_semaphore()
    pl.semaphore_signal(barrier, inc=1, device_id=partner, device_id_type=MESH)
    for axis in "xyz":
        for step in (1, 2, 3):
            pl.semaphore_signal(
                barrier, inc=1, device_id=device(axis, step), device_id_type=MESH
            )

    squares[...] = jnp.zeros_like(squares)

    def transposed(j):
        for t in range(2):
            xt[2 * j + t] = xv[j, :, t * TILE : (t + 1) * TILE].T

    def product(k, own, store):
        columns = pl.ds(column_of(k), WIDE)

        def tile(m, carry):
            block = jnp.dot(
                xt[4 * own + m], cv[:, columns], preferred_element_type=jnp.float32
            )
            for b in range(16):
                to = {
                    "x": b % 4,
                    "y": 2 * (m // 2) + (b // 4) % 2,
                    "z": 2 * (m % 2) + b // 8,
                }
                rel = {axis: (to[axis] - me[axis] + 4) % 4 for axis in "xyz"}
                for p, (first, second, third) in enumerate(ORDERS):
                    place = 16 * rel[first] + 4 * rel[second] + rel[third]
                    store(p, place, block[16 * b : 16 * b + 16, W * p : W * p + W])
            return carry

        lax.fori_loop(0, 4, tile, 0)

    def exchange(k):
        slot = k % 2

        def store(p, place, value):
            stage[slot, p, place] = value

        product(k, 0, store)
        pltpu.make_async_remote_copy(
            stage.at[slot], other.at[slot], stage_sem.at[slot], other_sem.at[slot],
            device_id=partner, device_id_type=MESH,
        ).start()

    def exchanged(k):
        slot = k % 2
        return pltpu.make_async_remote_copy(
            stage.at[slot], other.at[slot], stage_sem.at[slot], other_sem.at[slot],
            device_id=partner, device_id_type=MESH,
        )

    def send(u, at, size, to, sem, axis, step):
        pltpu.make_async_remote_copy(
            part.at[u, pl.ds(at, size)], to, send_sem.at[u], sem.at[u],
            device_id=device(axis, step), device_id_type=MESH,
        ).start()

    def arrived(u, what, sem):
        pltpu.make_async_remote_copy(
            what.at[u], what.at[u], send_sem.at[u], sem.at[u],
            device_id=partner, device_id_type=MESH,
        ).wait_recv()

    def ring_start(u, axis, size, fwd, fwd_sem, got, got_sem):
        half = size // 2
        send(u, 2 * size, half, fwd.at[u, 0], fwd_sem, axis, 1)
        send(u, 2 * size + half, half, fwd.at[u, 1], fwd_sem, axis, 3)
        send(u, size + half, half, got.at[u, 0, pl.ds(half, half)], got_sem, axis, 1)
        send(u, 3 * size, half, got.at[u, 1, pl.ds(0, half)], got_sem, axis, 3)

    def ring_forward(u, axis, size, fwd, fwd_sem, got, got_sem):
        half = size // 2
        arrived(u, fwd, fwd_sem)
        up, down = pl.ds(size, half), pl.ds(3 * size + half, half)
        part[u, up] = part[u, up] + fwd[u, 0]
        send(u, size, half, got.at[u, 0, pl.ds(0, half)], got_sem, axis, 1)
        part[u, down] = part[u, down] + fwd[u, 1]
        send(u, 3 * size + half, half, got.at[u, 1, pl.ds(half, half)], got_sem, axis, 3)

    def ring_end(u, size, got, got_sem):
        arrived(u, got, got_sem)
        mine = pl.ds(0, size)
        part[u, mine] = part[u, mine] + got[u, 0] + got[u, 1]

    def begin(k):
        slot = k % 2

        def store(p, place, value):
            part[unit_of(p, k), place] = value + other[slot, p, place]

        exchanged(k).wait_recv()
        product(k, 1, store)

    def stages(p, k, lag):
        axes = ORDERS[p]
        u = unit_of(p, k)
        if lag == 0:
            ring_start(u, axes[0], 16, fwd1, fwd1_sem, got1, got1_sem)
        elif lag == 1:
            ring_forward(u, axes[0], 16, fwd1, fwd1_sem, got1, got1_sem)
        elif lag == 2:
            ring_end(u, 16, got1, got1_sem)
            ring_start(u, axes[1], 4, fwd2, fwd2_sem, got2, got2_sem)
        elif lag == 3:
            ring_forward(u, axes[1], 4, fwd2, fwd2_sem, got2, got2_sem)
        elif lag == 4:
            ring_end(u, 4, got2, got2_sem)
            for step in (1, 3, 2):
                send(u, step, 1, got3.at[u, pl.ds(step - 1, 1)], got3_sem, axes[2], step)
        else:
            arrived(u, got3, got3_sem)
            final = part[u, 0] + got3[u, 0] + got3[u, 1] + got3[u, 2]
            grad[:, pl.ds(pl.multiple_of(column_of(k) + W * p, W), W)] = final
            squares[...] = squares[...] + final * final
            pltpu.make_async_remote_copy(
                part.at[u, pl.ds(0, 63)], part.at[u, pl.ds(0, 63)],
                send_sem.at[u], got3_sem.at[u],
                device_id=partner, device_id_type=MESH,
            ).wait_send()

    x_loads[0].wait()
    transposed(0)
    x_loads[1].wait()
    transposed(1)
    c_first.wait()
    product_slot = jnp.int32(0)

    def first_store(p, place, value):
        stage[0, p, place] = value

    product(product_slot, 0, first_store)
    pl.semaphore_wait(barrier, 10)
    exchanged(product_slot).start()
    x_loads[2].wait()
    x_loads[3].wait()
    c_rest.start()
    for load in state_loads:
        load.start()
    transposed(2)
    transposed(3)

    def step(k, carry):
        @pl.when(k < CHUNKS)
        def _():
            begin(k)

        for p in range(PORTIONS):

            @pl.when(k < COUNTS[p])
            def _():
                stages(p, k, 0)

        @pl.when(k == 0)
        def _():
            c_rest.wait()

        @pl.when(k + 1 < CHUNKS)
        def _():
            @pl.when(k >= 1)
            def _():
                exchanged(k - 1).wait_send()

            exchange(k + 1)

        for lag in range(1, LAGS):
            for p in range(PORTIONS):

                @pl.when((k >= lag) & (k - lag < COUNTS[p]))
                def _():
                    stages(p, k - lag, lag)

        return carry

    lax.fori_loop(0, CHUNKS + LAGS - 1, step, 0)
    exchanged(jnp.int32(CHUNKS - 2)).wait_send()
    exchanged(jnp.int32(CHUNKS - 1)).wait_send()

    total = squares[0:8] + squares[8:16]
    for at, axis in enumerate(("core", "x", "y", "z")):
        norm_out[at] = total
        targets = (
            [(0, partner)]
            if axis == "core"
            else [(step - 1, device(axis, step)) for step in (2, 1, 3)]
        )
        copies = [
            pltpu.make_async_remote_copy(
                norm_out.at[at], norm_in.at[at, place], norm_send.at[at, place],
                norm_recv.at[at, place], device_id=target, device_id_type=MESH,
            )
            for place, target in targets
        ]
        for copy in copies:
            copy.start()
        for (place, _), copy in zip(targets, copies):
            copy.wait_recv()
            total = total + norm_in[at, place]
        for copy in copies:
            copy.wait_send()

    limit = 0.5 * jnp.sqrt(jnp.float32(ROWS * D))
    whole = jnp.sum(total, keepdims=True)
    factor = limit / jnp.maximum(jnp.sqrt(whole), limit)
    for load in state_loads:
        load.wait()
    for c in range(0, D, 512):
        columns = slice(c, c + 512)
        scaled = factor * grad[:, columns]
        added = accum[:, columns] + scaled * scaled
        new_accum[:, columns] = added
        new_master[:, columns] = master[:, columns] - 0.5 * scaled / jnp.sqrt(added)


def shards(inputs, cotangent, master, accum):
    vmem, dma = pltpu.VMEM, pltpu.SemaphoreType.DMA
    f32, bf16 = jnp.float32, jnp.bfloat16
    return pl.pallas_call(
        kernel,
        out_shape=(
            jax.ShapeDtypeStruct((16, D), f32),
            jax.ShapeDtypeStruct((16, D), f32),
        ),
        in_specs=[pl.BlockSpec(memory_space=pl.ANY)] * 4,
        out_specs=(pl.BlockSpec(memory_space=vmem), pl.BlockSpec(memory_space=vmem)),
        scratch_shapes=[
            vmem((4, TOKENS, 512), bf16),
            vmem((8, TILE, TOKENS), bf16),
            vmem((TOKENS, D), bf16),
            vmem((2, PORTIONS, 64, 16, W), f32),
            vmem((2, PORTIONS, 64, 16, W), f32),
            vmem((UNITS, 64, 16, W), f32),
            vmem((UNITS, 2, 8, 16, W), f32),
            vmem((UNITS, 2, 16, 16, W), f32),
            vmem((UNITS, 2, 2, 16, W), f32),
            vmem((UNITS, 2, 4, 16, W), f32),
            vmem((UNITS, 3, 16, W), f32),
            vmem((16, D), f32),
            vmem((16, D), f32),
            vmem((16, D), f32),
            vmem((16, W), f32),
            vmem((4, 8, W), f32),
            vmem((4, 3, 8, W), f32),
            dma((4,)),
            dma((2,)),
            dma((2,)),
            dma((2,)),
            dma((2,)),
            dma((UNITS,)),
            dma((UNITS,)),
            dma((UNITS,)),
            dma((UNITS,)),
            dma((UNITS,)),
            dma((UNITS,)),
            dma((4, 3)),
            dma((4, 3)),
        ],
        compiler_params=pltpu.CompilerParams(
            collective_id=0, has_side_effects=True, vmem_limit_bytes=67_043_328
        ),
        name="gradient_step",
    )(inputs, cotangent, master, accum)


def solution(mesh):
    rows = P(("gx", "gy", "gz"), None)
    return jax.shard_map(
        shards, mesh=mesh, in_specs=(rows,) * 4, out_specs=(rows, rows), check_vma=False
    )
```

time: 358 us -> 121 us (0.34)
  waiting for transfers between devices: 251 us -> 0 us
  Pallas kernels: 0 us -> 117 us
  blocking collectives: 64.8 us -> 0 us
  matrix products: 25.3 us -> 0 us
  between operations: 14.8 us -> 0.64 us
    reduce_scatter x1 -> x0, waiting for transfers between devices: 251 us -> none  [shards(): lax.psum_scatter(lax.dot_general(inputs, cotangent, (((0,), (0,)), ((), (...]
    pallas_call x0 -> x1, Pallas kernels: none -> 117 us  [shards(): pl.pallas_call(kernel, out_shape=(jax.ShapeDtypeStruct((16, D), f32), jax...]
    psum x5 -> x0, blocking collectives: 35.9 us -> none  [one_axis_at_a_time(): return functools.reduce(lax.psum, axes, array)]
    all_to_all x1 -> x0, blocking collectives: 28.9 us -> none  [summed_on_arrival(): lax.all_to_all(parts, axis, split_axis=0, concat_axis=0, tiled=True)]
    dot_general x1 -> x0, matrix products: 25.3 us -> none  [shards(): lax.dot_general(inputs, cotangent, (((0,), (0,)), ((), ())), preferred_el...]
  transfers between devices with their start and end apart: 1 -> 0, of which waited for: 1 -> 0; matrix products, arithmetic and copies ran while one was open for 0% -> 0% of each run, Pallas kernels for 0% -> 0%
where the time goes in v1:
time: 121 us
  Pallas kernels  117 us (97%)
  local copies, waits for them, and re-layouts  3.34 us (3%)
    pallas_call x1, Pallas kernels, shards(): pl.pallas_call(kernel, out_shape=(jax.ShapeDtypeStruct((16, D), f32), jax...  117 us
    unnamed x2, local copies, waits for them, and re-layouts  3.34 us

profile of v1, /device:TPU:0, one launch (start us, length us, event | category | flops | bytes accessed | tf_op | source)
XLA Modules:
  0.0 120.8 jit_solution(10426896226086205874)
XLA Ops:
  0.6 116.9 %gradient_step.1 = (f32[16,4096]{1,0:T(8,128)}, f32[16,4096]{1,0:T(8,128)}) custom-call(bf16[1024,2048]{1,0:T(8,128)(2,1)} %x_hbm.1, bf16[1024,4096]{1,0:T(8,128)(2,1)} %c_hbm.1, f32[16,4096]{1,0:T(8,128)} %master_hbm.1, f32[16,4096]{1,0:T(8,128)} %accum_hbm.1), custom_call_target="tpu_custom_call" | custom-call | tf_op jit(solution)/shard_map/gradient_step/pallas_call | solution.py:297
  117.5 1.7 %copy.8 = f32[16,4096]{1,0:T(8,128)} copy(f32[16,4096]{1,0:T(8,128)} %get-tuple-element.4) | data formatting | bytes 524288
  119.2 1.7 %copy.9 = f32[16,4096]{1,0:T(8,128)} copy(f32[16,4096]{1,0:T(8,128)} %get-tuple-element.5) | data formatting | bytes 524288

commit v2 on v0

v2 whole, which is shorter than its diff:
```python
import jax
import jax.numpy as jnp
from jax import lax
from jax.experimental import pallas as pl
from jax.experimental.pallas import tpu as pltpu
from jax.sharding import PartitionSpec as P

MESH = pl.DeviceIdType.MESH

D = 4096
ROWS = 2048
TOKENS = 1024
W = 128
EACH = 4
WIDE = EACH * W
CHUNKS = D // WIDE
UNITS = D // W
TILE = 512
SLOTS = 4


def one_hot(axis):
    return ((axis + 2) % 3 // 2, (axis + 1) % 3 // 2, axis // 2)


def kernel(
    x_hbm, c_hbm,
    grad_hbm, factor_ref,
    xv, xt, cv, stage, other, part, fwd1, got1, fwd2, got2, got3,
    grad, squares, norm_out, norm_in1, norm_in2,
    x_sem, c_sem, grad_sem, stage_sem, other_sem, send_sem,
    fwd1_sem, got1_sem, fwd2_sem, got2_sem, got3_sem, norm_send, norm_recv,
):
    gx, gy, gz = lax.axis_index("gx"), lax.axis_index("gy"), lax.axis_index("gz")
    core = gx % 2
    me = (gz % 4, 2 * (gx // 2) + gz // 4, gy)

    def device(x, y, z, on):
        return (2 * (y // 2) + on, z, 4 * (y % 2) + x)

    def along(axis, step):
        x, y, z = ((at + step * hot) % 4 for at, hot in zip(me, one_hot(axis)))
        return device(x, y, z, core)

    partner = device(*me, 1 - core)

    x_loads = []
    for j in range(4):
        whose = 1 - core if j < 2 else core
        at = pl.multiple_of((j % 2) * 1024 + whose * 512, 512)
        x_loads.append(
            pltpu.make_async_copy(x_hbm.at[:, pl.ds(at, 512)], xv.at[j], x_sem.at[j])
        )
    c_first = pltpu.make_async_copy(
        c_hbm.at[:, pl.ds(0, WIDE)], cv.at[:, pl.ds(0, WIDE)], c_sem.at[0]
    )
    c_rest = pltpu.make_async_copy(
        c_hbm.at[:, pl.ds(WIDE, D - WIDE)], cv.at[:, pl.ds(WIDE, D - WIDE)], c_sem.at[1]
    )
    x_loads[0].start()
    c_first.start()
    x_loads[1].start()
    x_loads[2].start()
    x_loads[3].start()

    column = [
        (3 * on + step - 1, (me[0], me[1], (me[2] + step) % 4), (core + on) % 2)
        for step, on in ((2, 1), (2, 0), (1, 1), (3, 1), (1, 0), (3, 0), (4, 1))
    ]
    column = [(place, device(*at, on)) for place, at, on in column]
    plane = [
        (4 * a + b - 1 - (a > 0), device((me[0] + a) % 4, (me[1] + b) % 4, me[2], core))
        for a in (2, 1, 3, 0)
        for b in (2, 1, 3, 4)
        if (a, b) != (0, 4)
    ]
    barrier = pltpu.get_barrier_semaphore()
    for _, target in column + plane:
        pl.semaphore_signal(barrier, inc=1, device_id=target, device_id_type=MESH)

    squares[...] = jnp.zeros_like(squares)

    def transposed(j):
        xt[j] = xv[j].T

    def product(k, own, store):
        columns = pl.ds(pl.multiple_of(k * WIDE, WIDE), WIDE)
        hots = [one_hot((EACH * k + j) % 3) for j in range(EACH)]
        weights = [
            (16 * a + b + 4 * c, 4 * a + 16 * b + c, a + 4 * b + 16 * c)
            for a, b, c in hots
        ]

        def tile(m, carry):
            block = jnp.dot(
                xt[2 * own + m], cv[:, columns], preferred_element_type=jnp.float32
            )
            for j in range(EACH):
                wx, wy, wz = weights[j]
                xs = [wx * ((to - me[0] + 4) % 4) for to in range(4)]
                ys = [wy * ((2 * m + to - me[1] + 4) % 4) for to in range(2)]
                zs = [wz * ((to - me[2] + 4) % 4) for to in range(4)]
                for b in range(32):
                    place = xs[b % 4] + ys[b // 4 % 2] + zs[b // 8]
                    store(j, place, block[16 * b : 16 * b + 16, W * j : W * j + W])
            return carry

        lax.fori_loop(0, 2, tile, 0)

    def exchanged(k, j):
        slot, to = k % 2, k % SLOTS
        return pltpu.make_async_remote_copy(
            stage.at[slot, j], other.at[to, j], stage_sem.at[slot], other_sem.at[to, j],
            device_id=partner, device_id_type=MESH,
        )

    def exchange_product(k):
        def store(j, place, value):
            stage[k % 2, j, place] = value

        product(k, 0, store)

    def exchange(k):
        for j in range(EACH):
            exchanged(k, j).start()

    def exchange_sent(k):
        slot = k % 2
        pltpu.make_async_remote_copy(
            stage.at[slot], other.at[0], stage_sem.at[slot], other_sem.at[0, 0],
            device_id=partner, device_id_type=MESH,
        ).wait_send()

    def send(u, at, size, to, sem, target):
        pltpu.make_async_remote_copy(
            part.at[u, pl.ds(at, size)], to, send_sem.at[u], sem.at[u],
            device_id=target, device_id_type=MESH,
        ).start()

    def arrived(u, what, sem):
        pltpu.make_async_remote_copy(
            what.at[u], what.at[u], send_sem.at[u], sem.at[u],
            device_id=partner, device_id_type=MESH,
        ).wait_recv()

    def ring_start(u, axis, size, fwd, fwd_sem, got, got_sem):
        half = size // 2
        up, down = along(axis, 1), along(axis, 3)
        send(u, 2 * size, half, fwd.at[u, 0], fwd_sem, up)
        send(u, 2 * size + half, half, fwd.at[u, 1], fwd_sem, down)
        send(u, size + half, half, got.at[u, 0, pl.ds(half, half)], got_sem, up)
        send(u, 3 * size, half, got.at[u, 1, pl.ds(0, half)], got_sem, down)

    def ring_forward(u, axis, size, fwd, fwd_sem, got, got_sem):
        half = size // 2
        arrived(u, fwd, fwd_sem)
        up, down = pl.ds(size, half), pl.ds(3 * size + half, half)
        part[u, up] = part[u, up] + fwd[u, 0]
        part[u, down] = part[u, down] + fwd[u, 1]
        send(u, size, half, got.at[u, 0, pl.ds(0, half)], got_sem, along(axis, 1))
        send(u, 3 * size + half, half, got.at[u, 1, pl.ds(half, half)], got_sem, along(axis, 3))

    def ring_end(u, size, got, got_sem):
        arrived(u, got, got_sem)
        mine = pl.ds(0, size)
        part[u, mine] = part[u, mine] + got[u, 0] + got[u, 1]

    def start1(u):
        ring_start(u, u % 3, 16, fwd1, fwd1_sem, got1, got1_sem)

    def forward1(u):
        ring_forward(u, u % 3, 16, fwd1, fwd1_sem, got1, got1_sem)

    def start2(u):
        ring_end(u, 16, got1, got1_sem)
        ring_start(u, (u + 1) % 3, 4, fwd2, fwd2_sem, got2, got2_sem)

    def forward2(u):
        ring_forward(u, (u + 1) % 3, 4, fwd2, fwd2_sem, got2, got2_sem)

    def start3(u):
        ring_end(u, 4, got2, got2_sem)
        for step in (2, 1, 3):
            send(u, step, 1, got3.at[u, pl.ds(step - 1, 1)], got3_sem, along((u + 2) % 3, step))

    def end3(u):
        arrived(u, got3, got3_sem)
        final = part[u, 0] + got3[u, 0] + got3[u, 1] + got3[u, 2]
        grad[:, pl.ds(pl.multiple_of(u * W, W), W)] = final
        squares[...] = squares[...] + final * final
        pltpu.make_async_remote_copy(
            part.at[u, pl.ds(0, 63)], part.at[u, pl.ds(0, 63)],
            send_sem.at[u], got3_sem.at[u],
            device_id=partner, device_id_type=MESH,
        ).wait_send()

    def each(k, what):
        for j in range(EACH):
            what(EACH * k + j)

    zero, one = jnp.int32(0), jnp.int32(1)
    x_loads[0].wait()
    transposed(0)
    x_loads[1].wait()
    transposed(1)
    c_first.wait()
    exchange_product(zero)
    pl.semaphore_wait(barrier, 22)
    exchange(zero)
    x_loads[2].wait()
    transposed(2)
    x_loads[3].wait()
    transposed(3)
    c_rest.start()

    def first_store(j, place, value):
        part[j, place] = value

    product(zero, 1, first_store)
    for j in range(EACH):
        if j == 2:
            c_rest.wait()
            exchange_product(one)
            exchange(one)
        exchanged(zero, j).wait_recv()

        def add(i, carry, j=j):
            at = pl.ds(8 * i, 8)
            part[j, at] = part[j, at] + other[0, j, at]
            return carry

        lax.fori_loop(0, 8, add, 0)
        start1(jnp.int32(j))
    exchange_sent(zero)
    exchange_product(jnp.int32(2))
    exchange(jnp.int32(2))

    def step(k, carry):
        slot = k % SLOTS

        def store(j, place, value):
            part[EACH * k + j, place] = value + other[slot, j, place]

        for j in range(EACH):
            exchanged(k, j).wait_recv()
        product(k, 1, store)
        each(k, start1)

        @pl.when(k + 2 < CHUNKS)
        def _():
            exchange_sent(k)
            exchange_product(k + 2)
            exchange(k + 2)

        each(k - 1, forward1)

        @pl.when(k >= 3)
        def _():
            each(k - 3, start2)

        @pl.when(k >= 4)
        def _():
            each(k - 4, forward2)

        return carry

    lax.fori_loop(1, CHUNKS, step, 0)
    exchange_sent(CHUNKS - 2)
    exchange_sent(CHUNKS - 1)

    def all_of(low, high, what):
        def one_unit(u, carry):
            what(u)
            return carry

        lax.fori_loop(EACH * low, EACH * high, one_unit, 0)

    all_of(5, 6, start2)
    all_of(4, 5, forward2)
    all_of(7, 8, forward1)
    all_of(6, 7, start2)
    all_of(5, 6, forward2)
    all_of(0, 2, start3)
    all_of(7, 8, start2)
    all_of(6, 7, forward2)
    all_of(2, 4, start3)
    all_of(7, 8, forward2)
    all_of(4, 7, start3)
    all_of(0, 4, end3)
    all_of(7, 8, start3)
    all_of(4, 8, end3)

    to_hbm = pltpu.make_async_copy(grad, grad_hbm, grad_sem)
    to_hbm.start()

    total = squares[0:8] + squares[8:16]
    for level, (targets, inbox) in enumerate(((column, norm_in1), (plane, norm_in2))):
        norm_out[level] = total
        copies = [
            pltpu.make_async_remote_copy(
                norm_out.at[level], inbox.at[place], norm_send.at[level],
                norm_recv.at[level], device_id=target, device_id_type=MESH,
            )
            for place, target in targets
        ]
        for copy in copies:
            copy.start()
        whole = pltpu.make_async_remote_copy(
            inbox, inbox, norm_send.at[level], norm_recv.at[level],
            device_id=partner, device_id_type=MESH,
        )
        whole.wait_recv()
        for place, _ in targets:
            total = total + inbox[place]
        whole.wait_send()

    limit = 0.5 * jnp.sqrt(jnp.float32(ROWS * D))
    whole = jnp.sum(total, keepdims=True)
    factor = limit / jnp.maximum(jnp.sqrt(whole), limit)
    factor_ref[...] = jnp.broadcast_to(factor, factor_ref.shape)
    to_hbm.wait()


def shards(inputs, cotangent, master, accum):
    vmem, dma = pltpu.VMEM, pltpu.SemaphoreType.DMA
    f32, bf16 = jnp.float32, jnp.bfloat16
    gradient, factor = pl.pallas_call(
        kernel,
        out_shape=(
            jax.ShapeDtypeStruct((16, D), f32),
            jax.ShapeDtypeStruct((8, W), f32),
        ),
        in_specs=[pl.BlockSpec(memory_space=pl.ANY)] * 2,
        out_specs=(pl.BlockSpec(memory_space=pl.ANY), pl.BlockSpec(memory_space=vmem)),
        scratch_shapes=[
            vmem((4, TOKENS, 512), bf16),
            vmem((4, TILE, TOKENS), bf16),
            vmem((TOKENS, D), bf16),
            vmem((2, EACH, 64, 16, W), f32),
            vmem((SLOTS, EACH, 64, 16, W), f32),
            vmem((UNITS, 64, 16, W), f32),
            vmem((UNITS, 2, 8, 16, W), f32),
            vmem((UNITS, 2, 16, 16, W), f32),
            vmem((UNITS, 2, 2, 16, W), f32),
            vmem((UNITS, 2, 4, 16, W), f32),
            vmem((UNITS, 3, 16, W), f32),
            vmem((16, D), f32),
            vmem((16, W), f32),
            vmem((2, 8, W), f32),
            vmem((7, 8, W), f32),
            vmem((15, 8, W), f32),
            dma((4,)),
            dma((2,)),
            dma,
            dma((2,)),
            dma((SLOTS, EACH)),
            dma((UNITS,)),
            dma((UNITS,)),
            dma((UNITS,)),
            dma((UNITS,)),
            dma((UNITS,)),
            dma((UNITS,)),
            dma((2,)),
            dma((2,)),
        ],
        compiler_params=pltpu.CompilerParams(
            collective_id=0, has_side_effects=True, vmem_limit_bytes=67_043_328
        ),
        name="gradient_sum",
    )(inputs, cotangent)
    scaled = factor[0, 0] * gradient
    new_accum = accum + scaled * scaled
    new_master = master - 0.5 * scaled / jnp.sqrt(new_accum)
    return new_master, new_accum


def solution(mesh):
    rows = P(("gx", "gy", "gz"), None)
    return jax.shard_map(
        shards, mesh=mesh, in_specs=(rows,) * 4, out_specs=(rows, rows), check_vma=False
    )
```

time: 358 us -> 100 us (0.28)
  waiting for transfers between devices: 251 us -> 0 us
  Pallas kernels: 0 us -> 95.8 us
  blocking collectives: 64.8 us -> 0 us
  matrix products: 25.3 us -> 0 us
  between operations: 14.8 us -> 0.64 us
    reduce_scatter x1 -> x0, waiting for transfers between devices: 251 us -> none  [shards(): lax.psum_scatter(lax.dot_general(inputs, cotangent, (((0,), (0,)), ((), (...]
    pallas_call x0 -> x1, Pallas kernels: none -> 95.8 us  [shards(): pl.pallas_call(kernel, out_shape=(jax.ShapeDtypeStruct((16, D), f32), jax...]
    psum x5 -> x0, blocking collectives: 35.9 us -> none  [one_axis_at_a_time(): return functools.reduce(lax.psum, axes, array)]
    all_to_all x1 -> x0, blocking collectives: 28.9 us -> none  [summed_on_arrival(): lax.all_to_all(parts, axis, split_axis=0, concat_axis=0, tiled=True)]
    dot_general x1 -> x0, matrix products: 25.3 us -> none  [shards(): lax.dot_general(inputs, cotangent, (((0,), (0,)), ((), ())), preferred_el...]
  transfers between devices with their start and end apart: 1 -> 0, of which waited for: 1 -> 0; matrix products, arithmetic and copies ran while one was open for 0% -> 0% of each run, Pallas kernels for 0% -> 0%
where the time goes in v2:
time: 100 us
  Pallas kernels  95.8 us (96%)
  other arithmetic  2.5 us (2%)
  local copies, waits for them, and re-layouts  1.17 us (1%)
    pallas_call x1, Pallas kernels, shards(): pl.pallas_call(kernel, out_shape=(jax.ShapeDtypeStruct((16, D), f32), jax...  95.8 us
    sub x1, other arithmetic, shards(): new_master = master - 0.5 * scaled / jnp.sqrt(new_accum)  2.5 us

profile of v2, /device:TPU:0, one launch (start us, length us, event | category | flops | bytes accessed | tf_op | source)
XLA Modules:
  0.0 100.1 jit_solution(11138202407415816804)
XLA Ops:
  0.6 95.8 %gradient_sum.1 = (f32[16,4096]{1,0:T(8,128)}, f32[8,128]{1,0:T(8,128)}) custom-call(bf16[1024,2048]{1,0:T(8,128)(2,1)} %x_hbm.1, bf16[1024,4096]{1,0:T(8,128)(2,1)} %c_hbm.1), custom_call_target="tpu_custom_call" | custom-call | tf_op jit(solution)/shard_map/gradient_sum/pallas_call | solution.py:327
  96.5 1.2 %slice.3 = f32[1,1]{1,0:T(1,128)} slice(f32[8,128]{1,0:T(8,128)} %get-tuple-element.4), slice={[0:1], [0:1]} | slice | bytes 8 | tf_op jit(solution)/shard_map/slice | solution.py:371
  97.6 2.5 %multiply_subtract_fusion = (f32[16,4096]{1,0:T(8,128)}, f32[16,4096]{1,0:T(8,128)}) fusion(f32[16,4096]{1,0:T(8,128)} %param.6, f32[16,4096]{1,0:T(8,128)} %get-tuple-element.5, f32[]{:T(128)} %bitcast, f32[16,4096]{1,0:T(8,128)} %param.7), kind=kLoop, calls=%fused_computation | loop fusion | flops 393216 | bytes 1310724 | tf_op jit(solution)/shard_map/sub | solution.py:373

commit v3 on v2

v3 whole, which is shorter than its diff:
```python
import jax
import jax.numpy as jnp
from jax import lax
from jax.experimental import pallas as pl
from jax.experimental.pallas import tpu as pltpu
from jax.sharding import PartitionSpec as P

MESH = pl.DeviceIdType.MESH

D = 4096
ROWS = 2048
TOKENS = 1024
W = 128
EACH = 4
WIDE = EACH * W
CHUNKS = D // WIDE
UNITS = D // W
TILE = 512
SLOTS = 4
SENT = 8


def one_hot(axis):
    return ((axis + 2) % 3 // 2, (axis + 1) % 3 // 2, axis // 2)


def kernel(
    x_hbm, c_hbm,
    scaled_hbm,
    xv, xt, cv, stage, other, part, fwd1, got1, fwd2, got2, got3,
    grad, squares, norm_out, norm_in1, norm_in2,
    x_sem, c_sem, grad_sem, stage_sem, other_sem, send_sem,
    fwd1_sem, got1_sem, fwd2_sem, got2_sem, got3_sem, norm_send, norm_recv,
):
    gx, gy, gz = lax.axis_index("gx"), lax.axis_index("gy"), lax.axis_index("gz")
    core = gx % 2
    me = (gz % 4, 2 * (gx // 2) + gz // 4, gy)

    def device(x, y, z, on):
        return (2 * (y // 2) + on, z, 4 * (y % 2) + x)

    def along(axis, step):
        x, y, z = ((at + step * hot) % 4 for at, hot in zip(me, one_hot(axis)))
        return device(x, y, z, core)

    partner = device(*me, 1 - core)

    x_loads = []
    for j in range(4):
        whose = 1 - core if j < 2 else core
        at = pl.multiple_of((j % 2) * 1024 + whose * 512, 512)
        x_loads.append(
            pltpu.make_async_copy(x_hbm.at[:, pl.ds(at, 512)], xv.at[j], x_sem.at[j])
        )
    c_first = pltpu.make_async_copy(
        c_hbm.at[:, pl.ds(0, WIDE)], cv.at[:, pl.ds(0, WIDE)], c_sem.at[0]
    )
    c_second = pltpu.make_async_copy(
        c_hbm.at[:, pl.ds(WIDE, WIDE)], cv.at[:, pl.ds(WIDE, WIDE)], c_sem.at[1]
    )
    rest = pl.ds(2 * WIDE, D - 2 * WIDE)
    c_rest = pltpu.make_async_copy(c_hbm.at[:, rest], cv.at[:, rest], c_sem.at[2])
    x_loads[0].start()
    x_loads[1].start()
    c_first.start()

    column = [
        (3 * on + step - 1, (me[0], me[1], (me[2] + step) % 4), (core + on) % 2)
        for step, on in ((2, 1), (2, 0), (1, 1), (3, 1), (1, 0), (3, 0), (4, 1))
    ]
    column = [(place, device(*at, on)) for place, at, on in column]
    plane = [
        (4 * a + b - 1 - (a > 0), device((me[0] + a) % 4, (me[1] + b) % 4, me[2], core))
        for a in (2, 1, 3, 0)
        for b in (2, 1, 3, 4)
        if (a, b) != (0, 4)
    ]
    barrier = pltpu.get_barrier_semaphore()
    for _, target in column + plane:
        pl.semaphore_signal(barrier, inc=1, device_id=target, device_id_type=MESH)

    squares[...] = jnp.zeros_like(squares)

    def transposed(j):
        xt[j] = xv[j].T

    def product(k, own, store, js=range(EACH)):
        at = pl.multiple_of(k * WIDE + js[0] * W, len(js) * W)
        columns = pl.ds(at, len(js) * W)
        hots = [one_hot((EACH * k + j) % 3) for j in js]
        weights = [
            (32 * a + 2 * b + 8 * c, 8 * a + 32 * b + 2 * c, 2 * a + 8 * b + 32 * c)
            for a, b, c in hots
        ]

        def tile(m, carry):
            block = jnp.dot(
                xt[2 * own + m], cv[:, columns], preferred_element_type=jnp.float32
            )
            for i, j in enumerate(js):
                wx, wy, wz = weights[i]
                xs = [wx * ((to - me[0] + 4) % 4) for to in range(4)]
                ys = [wy * ((2 * m + to - me[1] + 4) % 4) for to in range(2)]
                zs = [wz * ((to - me[2] + 4) % 4) for to in range(4)]
                for b in range(32):
                    place = xs[b % 4] + ys[b // 4 % 2] + zs[b // 8]
                    value = block[16 * b : 16 * b + 16, W * i : W * i + W]
                    store(j, pl.ds(place, 2), value.reshape(2, 8, W))
            return carry

        lax.fori_loop(0, 2, tile, 0)

    def exchanged(k, j):
        slot, to = k % 2, k % SLOTS
        return pltpu.make_async_remote_copy(
            stage.at[slot, j], other.at[to, j], stage_sem.at[slot], other_sem.at[to, j],
            device_id=partner, device_id_type=MESH,
        )

    def exchange_product(k, js=range(EACH)):
        def store(j, place, value):
            stage[k % 2, j, place] = value

        product(k, 0, store, js)

    def exchange(k, js=range(EACH)):
        for j in js:
            exchanged(k, j).start()

    def exchange_sent(k):
        slot = k % 2
        pltpu.make_async_remote_copy(
            stage.at[slot], other.at[0], stage_sem.at[slot], other_sem.at[0, 0],
            device_id=partner, device_id_type=MESH,
        ).wait_send()

    def send(u, at, size, to, sem, target):
        pltpu.make_async_remote_copy(
            part.at[u, pl.ds(at, size)], to, send_sem.at[u // SENT], sem,
            device_id=target, device_id_type=MESH,
        ).start()

    def arrived(u, what, sem):
        pltpu.make_async_remote_copy(
            what.at[u], what.at[u], send_sem.at[0], sem,
            device_id=partner, device_id_type=MESH,
        ).wait_recv()

    def ring_start(u, axis, size, fwd, fwd_sem, got, got_sem):
        half = size // 2
        up, down = along(axis, 1), along(axis, 3)
        send(u, 2 * size, half, fwd.at[u, 0], fwd_sem, up)
        send(u, 2 * size + half, half, fwd.at[u, 1], fwd_sem, down)
        send(u, size + half, half, got.at[u, 0, pl.ds(half, half)], got_sem, up)
        send(u, 3 * size, half, got.at[u, 1, pl.ds(0, half)], got_sem, down)

    def ring_forward(u, axis, size, fwd, got, got_sem):
        half = size // 2
        up, down = pl.ds(size, half), pl.ds(3 * size + half, half)
        part[u, up] = part[u, up] + fwd[u, 0]
        part[u, down] = part[u, down] + fwd[u, 1]
        to_up, to_down = got.at[u, 0, pl.ds(0, half)], got.at[u, 1, pl.ds(half, half)]
        send(u, size, half, to_up, got_sem, along(axis, 1))
        send(u, 3 * size + half, half, to_down, got_sem, along(axis, 3))

    def ring_end(u, size, got):
        mine = pl.ds(0, size)
        part[u, mine] = part[u, mine] + got[u, 0] + got[u, 1]

    def chunk_arrived(k, what, sem):
        units = pl.ds(EACH * k, EACH)
        pltpu.make_async_remote_copy(
            what.at[units], what.at[units], send_sem.at[0], sem.at[k],
            device_id=partner, device_id_type=MESH,
        ).wait_recv()

    def units_of(k):
        return [EACH * k + j for j in range(EACH)]

    def start1(u):
        ring_start(u, u % 3, 32, fwd1, fwd1_sem.at[u], got1, got1_sem.at[u])

    def forward1(k, js=range(EACH)):
        for j in js:
            u = EACH * k + j
            arrived(u, fwd1, fwd1_sem.at[u])
            ring_forward(u, u % 3, 32, fwd1, got1, got1_sem.at[u])

    def start2(k):
        for u in units_of(k):
            arrived(u, got1, got1_sem.at[u])
            ring_end(u, 32, got1)
            ring_start(u, (u + 1) % 3, 8, fwd2, fwd2_sem.at[k], got2, got2_sem.at[k])

    def forward2(k):
        chunk_arrived(k, fwd2, fwd2_sem)
        for u in units_of(k):
            ring_forward(u, (u + 1) % 3, 8, fwd2, got2, got2_sem.at[k])

    def start3(k):
        chunk_arrived(k, got2, got2_sem)
        for u in units_of(k):
            ring_end(u, 8, got2)
            for step in (2, 1, 3):
                to = got3.at[u, step - 1]
                send(u, 2 * step, 2, to, got3_sem.at[k], along((u + 2) % 3, step))

    def end3(k):
        chunk_arrived(k, got3, got3_sem)
        for u in units_of(k):
            final = part[u, 0:2] + got3[u, 0] + got3[u, 1] + got3[u, 2]
            grad[:, pl.ds(pl.multiple_of(u * W, W), W)] = final.reshape(16, W)
            squares[...] = squares[...] + final * final

    def all_sent(i):
        sent = part.at[pl.ds(SENT * i, SENT), pl.ds(0, 126)]
        pltpu.make_async_remote_copy(
            sent, sent, send_sem.at[i], got3_sem.at[0],
            device_id=partner, device_id_type=MESH,
        ).wait_send()

    def own(k, js=range(EACH)):
        def store(j, place, value):
            part[EACH * k + j, place] = value

        product(k, 1, store, js)

    def exchange_ended(k, j):
        u, slot = EACH * k + j, k % SLOTS
        exchanged(k, j).wait_recv()

        def add(i, carry):
            at = pl.ds(pl.multiple_of(16 * i, 16), 16)
            part[u, at] = part[u, at] + other[slot, j, at]
            return carry

        lax.fori_loop(0, 8, add, 0)
        start1(u)

    low, high = range(2), range(2, 4)
    x_loads[0].wait()
    x_loads[2].start()
    x_loads[3].start()
    transposed(0)
    x_loads[1].wait()
    c_second.start()
    transposed(1)
    c_first.wait()
    exchange_product(0, low)
    pl.semaphore_wait(barrier, 22)
    exchange(0, low)
    exchange_product(0, high)
    exchange(0, high)
    x_loads[2].wait()
    transposed(2)
    x_loads[3].wait()
    transposed(3)
    c_second.wait()
    c_rest.start()
    own(0, low)
    exchange_ended(0, 0)
    exchange_ended(0, 1)
    own(0, high)
    exchange_ended(0, 2)
    exchange_ended(0, 3)
    exchange_product(1)
    exchange(1)
    own(1)
    forward1(0, low)
    exchange_ended(1, 0)
    exchange_ended(1, 1)
    forward1(0, high)
    c_rest.wait()
    exchange_sent(0)
    exchange_product(2)
    exchange(2)
    exchange_ended(1, 2)
    exchange_ended(1, 3)

    def step(k, carry):
        own(k)
        for j in range(EACH):
            exchange_ended(k, j)

        @pl.when(k == 2)
        def _():
            exchange_sent(1)
            exchange_product(3)
            exchange(3)

        forward1(k - 1)

        @pl.when(k + 2 < CHUNKS)
        def _():
            exchange_sent(k)
            exchange_product(k + 2)
            exchange(k + 2)

        @pl.when(k < 5)
        def _():
            start2(k - 2)

        @pl.when((k >= 4) & (k < 5))
        def _():
            forward2(k - 4)

        return carry

    lax.fori_loop(2, CHUNKS, step, 0)
    exchange_sent(CHUNKS - 2)
    exchange_sent(CHUNKS - 1)

    def all_of(low, high, what):
        if high - low == 1:
            what(low)
            return

        def one_chunk(k, carry):
            what(k)
            return carry

        lax.fori_loop(low, high, one_chunk, 0)

    all_of(7, 8, forward1)
    all_of(3, 6, start2)
    all_of(1, 3, forward2)
    all_of(6, 8, start2)
    all_of(3, 6, forward2)
    all_of(6, 8, forward2)
    all_of(0, 6, start3)
    all_of(6, 8, start3)
    all_of(0, 8, end3)

    total = squares[0] + squares[1]
    for level, (targets, inbox) in enumerate(((column, norm_in1), (plane, norm_in2))):
        norm_out[level] = total
        copies = [
            pltpu.make_async_remote_copy(
                norm_out.at[level], inbox.at[place], norm_send.at[level],
                norm_recv.at[level], device_id=target, device_id_type=MESH,
            )
            for place, target in targets
        ]
        for copy in copies:
            copy.start()
        whole = pltpu.make_async_remote_copy(
            inbox, inbox, norm_send.at[level], norm_recv.at[level],
            device_id=partner, device_id_type=MESH,
        )
        whole.wait_recv()
        for place, _ in targets:
            total = total + inbox[place]
        whole.wait_send()

    limit = 0.5 * jnp.sqrt(jnp.float32(ROWS * D))
    whole = jnp.sum(total, keepdims=True)
    factor = limit / jnp.maximum(jnp.sqrt(whole), limit)
    grad[...] = grad[...] * factor
    to_hbm = pltpu.make_async_copy(grad, scaled_hbm, grad_sem)
    to_hbm.start()
    for i in range(UNITS // SENT):
        all_sent(i)
    to_hbm.wait()


def shards(inputs, cotangent, master, accum):
    vmem, dma = pltpu.VMEM, pltpu.SemaphoreType.DMA
    f32, bf16 = jnp.float32, jnp.bfloat16
    scaled = pl.pallas_call(
        kernel,
        out_shape=jax.ShapeDtypeStruct((16, D), f32),
        in_specs=[pl.BlockSpec(memory_space=pl.ANY)] * 2,
        out_specs=pl.BlockSpec(memory_space=pl.ANY),
        scratch_shapes=[
            vmem((4, TOKENS, 512), bf16),
            vmem((4, TILE, TOKENS), bf16),
            vmem((TOKENS, D), bf16),
            vmem((2, EACH, 128, 8, W), f32),
            vmem((SLOTS, EACH, 128, 8, W), f32),
            vmem((UNITS, 128, 8, W), f32),
            vmem((UNITS, 2, 16, 8, W), f32),
            vmem((UNITS, 2, 32, 8, W), f32),
            vmem((UNITS, 2, 4, 8, W), f32),
            vmem((UNITS, 2, 8, 8, W), f32),
            vmem((UNITS, 3, 2, 8, W), f32),
            vmem((16, D), f32),
            vmem((2, 8, W), f32),
            vmem((2, 8, W), f32),
            vmem((7, 8, W), f32),
            vmem((15, 8, W), f32),
            dma((4,)),
            dma((3,)),
            dma,
            dma((2,)),
            dma((SLOTS, EACH)),
            dma((UNITS // SENT,)),
            dma((UNITS,)),
            dma((UNITS,)),
            dma((CHUNKS,)),
            dma((CHUNKS,)),
            dma((CHUNKS,)),
            dma((2,)),
            dma((2,)),
        ],
        compiler_params=pltpu.CompilerParams(
            collective_id=0, has_side_effects=True, vmem_limit_bytes=64_000_000
        ),
        name="gradient_sum",
    )(inputs, cotangent)
    new_accum = accum + scaled * scaled
    new_master = master - 0.5 * scaled / jnp.sqrt(new_accum)
    return new_master, new_accum


def solution(mesh):
    rows = P(("gx", "gy", "gz"), None)
    return jax.shard_map(
        shards, mesh=mesh, in_specs=(rows,) * 4, out_specs=(rows, rows), check_vma=False
    )
```

time: 100 us -> 90.4 us (0.904)
  Pallas kernels: 95.8 us -> 87.8 us
  local copies, waits for them, and re-layouts: 1.17 us -> 0.01 us
    pallas_call x1, Pallas kernels: 95.8 us -> 87.8 us  [shards(): pl.pallas_call(kernel, out_shape=jax.ShapeDtypeStruct((16, D), f32), in_s...]
    slice x1 -> x0, local copies, waits for them, and re-layouts: 1.17 us -> none  [shards(): scaled = factor[0, 0] * gradient]
where the time goes in v3:
time: 90.4 us; the launch traced here: 90.2 us
  Pallas kernels  87.8 us (97%)
  other arithmetic  1.81 us (2%)
    pallas_call x1, Pallas kernels, shards(): pl.pallas_call(kernel, out_shape=jax.ShapeDtypeStruct((16, D), f32), in_s...  87.8 us

profile of v3, /device:TPU:0, one launch (start us, length us, event | category | flops | bytes accessed | tf_op | source)
XLA Modules:
  0.0 90.2 jit_solution(10276337293934068948)
XLA Ops:
  0.6 0.0 copy-start.1
  0.6 0.0 copy-start
  0.7 87.8 %gradient_sum.1 = f32[16,4096]{1,0:T(8,128)} custom-call(bf16[1024,2048]{1,0:T(8,128)(2,1)} %x_hbm.1, bf16[1024,4096]{1,0:T(8,128)(2,1)} %c_hbm.1), custom_call_target="tpu_custom_call" | custom-call | tf_op jit(solution)/shard_map/gradient_sum/pallas_call | solution.py:369
  88.4 0.0 copy-done.1
  88.4 0.0 copy-done
  88.4 1.8 %multiply_subtract_fusion = (f32[16,4096]{1,0:T(8,128)}, f32[16,4096]{1,0:T(8,128)}) fusion(f32[16,4096]{1,0:T(8,128)S(1)} %copy-done, f32[16,4096]{1,0:T(8,128)} %gradient_sum.1, f32[16,4096]{1,0:T(8,128)S(1)} %copy-done.1), kind=kLoop, calls=%fused_computation | loop fusion | flops 327680 | bytes 1310720 | tf_op jit(solution)/shard_map/sub | solution.py:411
Async XLA Ops:
  0.6 87.8 %copy-start.1 = (f32[16,4096]{1,0:T(8,128)S(1)}, f32[16,4096]{1,0:T(8,128)}, u32[]{:S(2)}) copy-start(f32[16,4096]{1,0:T(8,128)} %param.7) | copy-start | bytes 786436
  0.6 87.8 %copy-start = (f32[16,4096]{1,0:T(8,128)S(1)}, f32[16,4096]{1,0:T(8,128)}, u32[]{:S(2)}) copy-start(f32[16,4096]{1,0:T(8,128)} %param.6) | copy-start | bytes 786436

commit v4 on v3

--- a/solution.py
+++ b/solution.py
@@ -24,12 +24,18 @@
     return ((axis + 2) % 3 // 2, (axis + 1) % 3 // 2, axis // 2)
 
 
+def axes_of(u):
+    first = u % 3
+    spare = u // 8 % 2 * (1 - u // 16) * one_hot(first)[0]
+    return first, (first + 1 + spare) % 3, (first + 2 - spare) % 3
+
+
 def kernel(
     x_hbm, c_hbm,
-    scaled_hbm,
+    scaled_ref,
     xv, xt, cv, stage, other, part, fwd1, got1, fwd2, got2, got3,
     grad, squares, norm_out, norm_in1, norm_in2,
-    x_sem, c_sem, grad_sem, stage_sem, other_sem, send_sem,
+    x_sem, c_sem, stage_sem, other_sem, send_sem,
     fwd1_sem, got1_sem, fwd2_sem, got2_sem, got3_sem, norm_send, norm_recv,
 ):
     gx, gy, gz = lax.axis_index("gx"), lax.axis_index("gy"), lax.axis_index("gz")
@@ -50,19 +56,20 @@
         whose = 1 - core if j < 2 else core
         at = pl.multiple_of((j % 2) * 1024 + whose * 512, 512)
         x_loads.append(
-            pltpu.make_async_copy(x_hbm.at[:, pl.ds(at, 512)], xv.at[j], x_sem.at[j])
+            pltpu.make_async_copy(x_hbm.at[:, pl.ds(at, 512)], xv.at[j % 2], x_sem.at[j])
         )
-    c_first = pltpu.make_async_copy(
-        c_hbm.at[:, pl.ds(0, WIDE)], cv.at[:, pl.ds(0, WIDE)], c_sem.at[0]
-    )
+    c_first, c_next = [
+        pltpu.make_async_copy(c_hbm.at[:, at], cv.at[:, at], c_sem.at[i])
+        for i, at in ((0, pl.ds(0, 2 * W)), (3, pl.ds(2 * W, 2 * W)))
+    ]
     c_second = pltpu.make_async_copy(
         c_hbm.at[:, pl.ds(WIDE, WIDE)], cv.at[:, pl.ds(WIDE, WIDE)], c_sem.at[1]
     )
     rest = pl.ds(2 * WIDE, D - 2 * WIDE)
     c_rest = pltpu.make_async_copy(c_hbm.at[:, rest], cv.at[:, rest], c_sem.at[2])
     x_loads[0].start()
+    c_first.start()
     x_loads[1].start()
-    c_first.start()
 
     column = [
         (3 * on + step - 1, (me[0], me[1], (me[2] + step) % 4), (core + on) % 2)
@@ -82,15 +89,14 @@
     squares[...] = jnp.zeros_like(squares)
 
     def transposed(j):
-        xt[j] = xv[j].T
+        xt[j] = xv[j % 2].T
 
     def product(k, own, store, js=range(EACH)):
         at = pl.multiple_of(k * WIDE + js[0] * W, len(js) * W)
         columns = pl.ds(at, len(js) * W)
-        hots = [one_hot((EACH * k + j) % 3) for j in js]
+        hots = [[one_hot(axis) for axis in axes_of(EACH * k + j)] for j in js]
         weights = [
-            (32 * a + 2 * b + 8 * c, 8 * a + 32 * b + 2 * c, 2 * a + 8 * b + 32 * c)
-            for a, b, c in hots
+            [32 * a + 8 * b + 2 * c for a, b, c in zip(*of_unit)] for of_unit in hots
         ]
 
         def tile(m, carry):
@@ -108,7 +114,7 @@
                     store(j, pl.ds(place, 2), value.reshape(2, 8, W))
             return carry
 
-        lax.fori_loop(0, 2, tile, 0)
+        lax.fori_loop(0, 2, tile, 0, unroll=len(js) < EACH)
 
     def exchanged(k, j):
         slot, to = k % 2, k % SLOTS
@@ -139,12 +145,6 @@
             part.at[u, pl.ds(at, size)], to, send_sem.at[u // SENT], sem,
             device_id=target, device_id_type=MESH,
         ).start()
-
-    def arrived(u, what, sem):
-        pltpu.make_async_remote_copy(
-            what.at[u], what.at[u], send_sem.at[0], sem,
-            device_id=partner, device_id_type=MESH,
-        ).wait_recv()
 
     def ring_start(u, axis, size, fwd, fwd_sem, got, got_sem):
         half = size // 2
@@ -178,24 +178,29 @@
         return [EACH * k + j for j in range(EACH)]
 
     def start1(u):
-        ring_start(u, u % 3, 32, fwd1, fwd1_sem.at[u], got1, got1_sem.at[u])
+        ring_start(u, u % 3, 32, fwd1, fwd1_sem.at[u // 2], got1, got1_sem.at[u // EACH])
 
     def forward1(k, js=range(EACH)):
         for j in js:
             u = EACH * k + j
-            arrived(u, fwd1, fwd1_sem.at[u])
-            ring_forward(u, u % 3, 32, fwd1, got1, got1_sem.at[u])
+            if j % 2 == 0:
+                pair = fwd1.at[pl.ds(u, 2)]
+                pltpu.make_async_remote_copy(
+                    pair, pair, send_sem.at[0], fwd1_sem.at[u // 2],
+                    device_id=partner, device_id_type=MESH,
+                ).wait_recv()
+            ring_forward(u, u % 3, 32, fwd1, got1, got1_sem.at[k])
 
     def start2(k):
+        chunk_arrived(k, got1, got1_sem)
         for u in units_of(k):
-            arrived(u, got1, got1_sem.at[u])
             ring_end(u, 32, got1)
-            ring_start(u, (u + 1) % 3, 8, fwd2, fwd2_sem.at[k], got2, got2_sem.at[k])
+            ring_start(u, axes_of(u)[1], 8, fwd2, fwd2_sem.at[k], got2, got2_sem.at[k])
 
     def forward2(k):
         chunk_arrived(k, fwd2, fwd2_sem)
         for u in units_of(k):
-            ring_forward(u, (u + 1) % 3, 8, fwd2, got2, got2_sem.at[k])
+            ring_forward(u, axes_of(u)[1], 8, fwd2, got2, got2_sem.at[k])
 
     def start3(k):
         chunk_arrived(k, got2, got2_sem)
@@ -203,7 +208,7 @@
             ring_end(u, 8, got2)
             for step in (2, 1, 3):
                 to = got3.at[u, step - 1]
-                send(u, 2 * step, 2, to, got3_sem.at[k], along((u + 2) % 3, step))
+                send(u, 2 * step, 2, to, got3_sem.at[k], along(axes_of(u)[2], step))
 
     def end3(k):
         chunk_arrived(k, got3, got3_sem)
@@ -239,16 +244,18 @@
 
     low, high = range(2), range(2, 4)
     x_loads[0].wait()
+    transposed(0)
     x_loads[2].start()
-    x_loads[3].start()
-    transposed(0)
     x_loads[1].wait()
+    c_next.start()
     c_second.start()
     transposed(1)
+    x_loads[3].start()
     c_first.wait()
     exchange_product(0, low)
     pl.semaphore_wait(barrier, 22)
     exchange(0, low)
+    c_next.wait()
     exchange_product(0, high)
     exchange(0, high)
     x_loads[2].wait()
@@ -260,22 +267,27 @@
     own(0, low)
     exchange_ended(0, 0)
     exchange_ended(0, 1)
+    exchange_product(1, low)
+    exchange(1, low)
     own(0, high)
     exchange_ended(0, 2)
     exchange_ended(0, 3)
-    exchange_product(1)
-    exchange(1)
-    own(1)
-    forward1(0, low)
+    exchange_product(1, high)
+    exchange(1, high)
+    own(1, low)
     exchange_ended(1, 0)
     exchange_ended(1, 1)
-    forward1(0, high)
     c_rest.wait()
     exchange_sent(0)
-    exchange_product(2)
-    exchange(2)
+    exchange_product(2, low)
+    exchange(2, low)
+    forward1(0, low)
+    own(1, high)
     exchange_ended(1, 2)
     exchange_ended(1, 3)
+    exchange_product(2, high)
+    exchange(2, high)
+    forward1(0, high)
 
     def step(k, carry):
         own(k)
@@ -355,12 +367,9 @@
     limit = 0.5 * jnp.sqrt(jnp.float32(ROWS * D))
     whole = jnp.sum(total, keepdims=True)
     factor = limit / jnp.maximum(jnp.sqrt(whole), limit)
-    grad[...] = grad[...] * factor
-    to_hbm = pltpu.make_async_copy(grad, scaled_hbm, grad_sem)
-    to_hbm.start()
     for i in range(UNITS // SENT):
         all_sent(i)
-    to_hbm.wait()
+    scaled_ref[...] = grad[...] * factor
 
 
 def shards(inputs, cotangent, master, accum):
@@ -368,11 +377,11 @@
     f32, bf16 = jnp.float32, jnp.bfloat16
     scaled = pl.pallas_call(
         kernel,
-        out_shape=jax.ShapeDtypeStruct((16, D), f32),
+        out_shape=vmem((16, D), f32),
         in_specs=[pl.BlockSpec(memory_space=pl.ANY)] * 2,
-        out_specs=pl.BlockSpec(memory_space=pl.ANY),
+        out_specs=pl.BlockSpec(memory_space=vmem),
         scratch_shapes=[
-            vmem((4, TOKENS, 512), bf16),
+            vmem((2, TOKENS, 512), bf16),
             vmem((4, TILE, TOKENS), bf16),
             vmem((TOKENS, D), bf16),
             vmem((2, EACH, 128, 8, W), f32),
@@ -389,13 +398,12 @@
             vmem((7, 8, W), f32),
             vmem((15, 8, W), f32),
             dma((4,)),
-            dma((3,)),
-            dma,
+            dma((4,)),
             dma((2,)),
             dma((SLOTS, EACH)),
             dma((UNITS // SENT,)),
-            dma((UNITS,)),
-            dma((UNITS,)),
+            dma((UNITS // 2,)),
+            dma((CHUNKS,)),
             dma((CHUNKS,)),
             dma((CHUNKS,)),
             dma((CHUNKS,)),

time: 90.4 us -> 87.6 us (0.969)
  Pallas kernels: 87.8 us -> 86 us
  other arithmetic: 1.81 us -> 0.84 us
    pallas_call x1, Pallas kernels: 87.8 us -> 86 us  [shards(): pl.pallas_call(kernel, out_shape=vmem((16, D), f32), in_specs=[pl.BlockSp...]
    sub x1, other arithmetic: 1.81 us -> 0.84 us  [shards(): new_master = master - 0.5 * scaled / jnp.sqrt(new_accum)]
where the time goes in v4:
time: 87.6 us; the launch traced here: 87.5 us
  Pallas kernels  86 us (98%)
    pallas_call x1, Pallas kernels, shards(): pl.pallas_call(kernel, out_shape=vmem((16, D), f32), in_specs=[pl.BlockSp...  86 us

profile of v4, /device:TPU:0, one launch (start us, length us, event | category | flops | bytes accessed | tf_op | source)
XLA Modules:
  0.0 87.5 jit_solution(3561925993551831166)
XLA Ops:
  0.6 0.0 copy-start.1
  0.6 0.0 copy-start
  0.7 86.0 %gradient_sum.1 = f32[16,4096]{1,0:T(8,128)S(1)} custom-call(bf16[1024,2048]{1,0:T(8,128)(2,1)} %x_hbm.1, bf16[1024,4096]{1,0:T(8,128)(2,1)} %c_hbm.1), custom_call_target="tpu_custom_call" | custom-call | tf_op jit(solution)/shard_map/gradient_sum/pallas_call | solution.py:378
  86.6 0.0 copy-done.1
  86.6 0.0 copy-done
  86.6 0.8 multiply_subtract_fusion
Async XLA Ops:
  0.6 86.0 %copy-start.1 = (f32[16,4096]{1,0:T(8,128)S(1)}, f32[16,4096]{1,0:T(8,128)}, u32[]{:S(2)}) copy-start(f32[16,4096]{1,0:T(8,128)} %param.7) | copy-start | bytes 786436
  0.6 86.0 %copy-start = (f32[16,4096]{1,0:T(8,128)S(1)}, f32[16,4096]{1,0:T(8,128)}, u32[]{:S(2)}) copy-start(f32[16,4096]{1,0:T(8,128)} %param.6) | copy-start | bytes 786436

commit v5 on v4

--- a/solution.py
+++ b/solution.py
@@ -25,15 +25,13 @@
 
 
 def axes_of(u):
-    first = u % 3
-    spare = u // 8 % 2 * (1 - u // 16) * one_hot(first)[0]
-    return first, (first + 1 + spare) % 3, (first + 2 - spare) % 3
+    return u % 3, (u + 1) % 3, (u + 2) % 3
 
 
 def kernel(
     x_hbm, c_hbm,
     scaled_ref,
-    xv, xt, cv, stage, other, part, fwd1, got1, fwd2, got2, got3,
+    xv, cv, stage, other, part, fwd1, got1, fwd2, got2, got3,
     grad, squares, norm_out, norm_in1, norm_in2,
     x_sem, c_sem, stage_sem, other_sem, send_sem,
     fwd1_sem, got1_sem, fwd2_sem, got2_sem, got3_sem, norm_send, norm_recv,
@@ -56,7 +54,7 @@
         whose = 1 - core if j < 2 else core
         at = pl.multiple_of((j % 2) * 1024 + whose * 512, 512)
         x_loads.append(
-            pltpu.make_async_copy(x_hbm.at[:, pl.ds(at, 512)], xv.at[j % 2], x_sem.at[j])
+            pltpu.make_async_copy(x_hbm.at[:, pl.ds(at, 512)], xv.at[j], x_sem.at[j])
         )
     c_first, c_next = [
         pltpu.make_async_copy(c_hbm.at[:, at], cv.at[:, at], c_sem.at[i])
@@ -89,7 +87,7 @@
     squares[...] = jnp.zeros_like(squares)
 
     def transposed(j):
-        xt[j] = xv[j % 2].T
+        pass
 
     def product(k, own, store, js=range(EACH)):
         at = pl.multiple_of(k * WIDE + js[0] * W, len(js) * W)
@@ -100,8 +98,9 @@
         ]
 
         def tile(m, carry):
-            block = jnp.dot(
-                xt[2 * own + m], cv[:, columns], preferred_element_type=jnp.float32
+            block = lax.dot_general(
+                xv[2 * own + m], cv[:, columns], (((0,), (0,)), ((), ())),
+                preferred_element_type=jnp.float32,
             )
             for i, j in enumerate(js):
                 wx, wy, wz = weights[i]
@@ -146,13 +145,15 @@
             device_id=target, device_id_type=MESH,
         ).start()
 
-    def ring_start(u, axis, size, fwd, fwd_sem, got, got_sem):
+    def ring_start(u, axis, size, fwd, fwd_sem, got, got_sem, now=(0, 1)):
         half = size // 2
         up, down = along(axis, 1), along(axis, 3)
-        send(u, 2 * size, half, fwd.at[u, 0], fwd_sem, up)
-        send(u, 2 * size + half, half, fwd.at[u, 1], fwd_sem, down)
-        send(u, size + half, half, got.at[u, 0, pl.ds(half, half)], got_sem, up)
-        send(u, 3 * size, half, got.at[u, 1, pl.ds(0, half)], got_sem, down)
+        if 0 in now:
+            send(u, 2 * size, half, fwd.at[u, 0], fwd_sem, up)
+            send(u, 2 * size + half, half, fwd.at[u, 1], fwd_sem, down)
+        if 1 in now:
+            send(u, size + half, half, got.at[u, 0, pl.ds(half, half)], got_sem, up)
+            send(u, 3 * size, half, got.at[u, 1, pl.ds(0, half)], got_sem, down)
 
     def ring_forward(u, axis, size, fwd, got, got_sem):
         half = size // 2
@@ -177,8 +178,9 @@
     def units_of(k):
         return [EACH * k + j for j in range(EACH)]
 
-    def start1(u):
-        ring_start(u, u % 3, 32, fwd1, fwd1_sem.at[u // 2], got1, got1_sem.at[u // EACH])
+    def start1(u, now=(0, 1)):
+        sems = fwd1_sem.at[u // 2], got1_sem.at[u // EACH]
+        ring_start(u, u % 3, 32, fwd1, sems[0], got1, sems[1], now)
 
     def forward1(k, js=range(EACH)):
         for j in js:
@@ -193,9 +195,12 @@
 
     def start2(k):
         chunk_arrived(k, got1, got1_sem)
-        for u in units_of(k):
-            ring_end(u, 32, got1)
-            ring_start(u, axes_of(u)[1], 8, fwd2, fwd2_sem.at[k], got2, got2_sem.at[k])
+        for now in (0, 1):
+            for u in units_of(k):
+                if now == 0:
+                    ring_end(u, 32, got1)
+                sems = fwd2_sem.at[k], got2_sem.at[k]
+                ring_start(u, axes_of(u)[1], 8, fwd2, sems[0], got2, sems[1], (now,))
 
     def forward2(k):
         chunk_arrived(k, fwd2, fwd2_sem)
@@ -230,7 +235,7 @@
 
         product(k, 1, store, js)
 
-    def exchange_ended(k, j):
+    def exchange_ended(k, j, now=(0, 1)):
         u, slot = EACH * k + j, k % SLOTS
         exchanged(k, j).wait_recv()
 
@@ -240,7 +245,7 @@
             return carry
 
         lax.fori_loop(0, 8, add, 0)
-        start1(u)
+        start1(u, now)
 
     low, high = range(2), range(2, 4)
     x_loads[0].wait()
@@ -292,7 +297,9 @@
     def step(k, carry):
         own(k)
         for j in range(EACH):
-            exchange_ended(k, j)
+            exchange_ended(k, j, (0,))
+        for j in range(EACH):
+            start1(EACH * k + j, (1,))
 
         @pl.when(k == 2)
         def _():
@@ -381,8 +388,7 @@
         in_specs=[pl.BlockSpec(memory_space=pl.ANY)] * 2,
         out_specs=pl.BlockSpec(memory_space=vmem),
         scratch_shapes=[
-            vmem((2, TOKENS, 512), bf16),
-            vmem((4, TILE, TOKENS), bf16),
+            vmem((4, TOKENS, 512), bf16),
             vmem((TOKENS, D), bf16),
             vmem((2, EACH, 128, 8, W), f32),
             vmem((SLOTS, EACH, 128, 8, W), f32),

time: 87.6 us -> 87.2 us (level)
  no operation moved by 1% of the time
where the time goes in v5:
time: 87.2 us; the launch traced here: 87.1 us
  Pallas kernels  85.6 us (98%)
    pallas_call x1, Pallas kernels, shards(): pl.pallas_call(kernel, out_shape=vmem((16, D), f32), in_specs=[pl.BlockSp...  85.6 us

profile of v5, /device:TPU:0, one launch (start us, length us, event | category | flops | bytes accessed | tf_op | source)
XLA Modules:
  0.0 87.1 jit_solution(2966621451211403198)
XLA Ops:
  0.6 0.0 copy-start.1
  0.6 0.0 copy-start
  0.7 85.6 %gradient_sum.1 = f32[16,4096]{1,0:T(8,128)S(1)} custom-call(bf16[1024,2048]{1,0:T(8,128)(2,1)} %x_hbm.1, bf16[1024,4096]{1,0:T(8,128)(2,1)} %c_hbm.1), custom_call_target="tpu_custom_call" | custom-call | tf_op jit(solution)/shard_map/gradient_sum/pallas_call | solution.py:385
  86.2 0.0 copy-done.1
  86.2 0.0 copy-done
  86.2 0.8 multiply_subtract_fusion
Async XLA Ops:
  0.6 85.6 %copy-start.1 = (f32[16,4096]{1,0:T(8,128)S(1)}, f32[16,4096]{1,0:T(8,128)}, u32[]{:S(2)}) copy-start(f32[16,4096]{1,0:T(8,128)} %param.7) | copy-start | bytes 786436
  0.6 85.6 %copy-start = (f32[16,4096]{1,0:T(8,128)S(1)}, f32[16,4096]{1,0:T(8,128)}, u32[]{:S(2)}) copy-start(f32[16,4096]{1,0:T(8,128)} %param.6) | copy-start | bytes 786436
